TPU v7x, 32 devices: a whole 2x2x4 slice. The times are simulated.
32 devices in a mesh: obs: 8 (over z, x), chan: 4 (over y, core).
Axes of the slice: x: 2, y: 2, z: 4, core: 2. Of those that a mesh axis runs over, the one named last changes fastest.
Arguments:
- departures: bfloat16 [8192, 16384], P('chan', 'obs'), may hold values from -8 to 8
- predictors: bfloat16 [10, 16384], P(None, 'obs'), may hold values from -3 to 3
- inv_band: bfloat16 [63, 8192], P(None, 'chan'), may hold values from -1 to 2.5
- band_id: int32 [8192], replicated, may hold values from 0 to 340, never falling along the last dimension, each value on 1 to 32 neighbouring positions
- line_counts: int32 [128], P('obs'), may hold values from 24 to 128
Outputs:
- gram: float32 [100, 8192], P(None, ('chan', 'obs'))
- rhs: float32 [10, 8192], P(None, ('chan', 'obs'))
Inputs may be any that keep to these rules, and one draw needn't show every extreme that they name: `band_id`: band numbers never fall along the channels; a band spans 1 to 32 channels. `line_counts`: slots of a scan line at or beyond its count are empty.
All inputs are finite; a program needn't handle non-finite values.
Results may differ from a plain program's by a relative error of at most 0.00062.
Values may be sent and summed in bfloat16 or wider, within the bound.
A program may use at most 64 MiB of HBM per device.

v0:
```python
import jax
import jax.numpy as jnp
import numpy as np
from jax import lax
from jax.sharding import PartitionSpec as P

huber_edge = 1.0


def with_halo(cells, sides, width):
    for axis, dim in sides:
        count = lax.axis_size(axis)
        ends = count - 1
        head = lax.slice_in_dim(cells, 0, width, axis=dim)
        tail = lax.slice_in_dim(cells, cells.shape[dim] - width, cells.shape[dim], axis=dim)
        cells = jnp.concatenate(
            [
                lax.ppermute(tail, axis, [(i, (i + 1) % count) for i in range(ends)]),
                cells,
                lax.ppermute(head, axis, [((i + 1) % count, i) for i in range(ends)]),
            ],
            axis=dim,
        )
    return cells


def upper_tables(count):
    firsts = []
    seconds = []
    for first in range(count):
        for second in range(first, count):
            firsts.append(first)
            seconds.append(second)
    mirror = []
    for first in range(count):
        for second in range(count):
            low = min(first, second)
            high = max(first, second)
            mirror.append(low * count - low * (low - 1) // 2 + high - low)
    return (np.array(firsts), np.array(seconds), np.array(mirror))


def on_device(departures, predictors, inv_band, band_id, line_counts):
    own, obs_dev = departures.shape
    count_pred = predictors.shape[0]
    half = inv_band.shape[0] // 2
    tile = min(256, own)
    tiles = own // tile
    extent = tile + 2 * half
    padded = with_halo(departures, (("chan", 0),), half)
    base = lax.axis_index("chan") * own
    marked = jnp.pad(band_id, (half, half), constant_values=-1)
    near_all = lax.dynamic_slice_in_dim(marked, base, own + 2 * half)
    line_slots = obs_dev // line_counts.shape[0]
    live = (
        (jnp.arange(line_slots, dtype=jnp.int32)[None, :] < line_counts[:, None])
        .reshape(obs_dev)
        .astype(jnp.float32)
    )
    band_rows = inv_band.T.reshape(tiles, tile, 2 * half + 1)
    widened = jnp.pad(band_rows, ((0, 0), (0, 0), (0, extent + 1 - (2 * half + 1))))
    skewed = widened.reshape(tiles, tile * (extent + 1))[:, : tile * extent].reshape(
        tiles, tile, extent
    )
    pieces = []
    for number in range(tiles):
        own_ids = near_all[half + number * tile : half + (number + 1) * tile]
        near_ids = near_all[number * tile : number * tile + extent]
        same = own_ids[:, None] == near_ids[None, :]
        matrix = jnp.where(same, skewed[number], jnp.zeros_like(skewed[number]))
        window = padded[number * tile : number * tile + extent]
        pieces.append(jnp.dot(matrix, window, preferred_element_type=jnp.float32))
    weighted = jnp.concatenate(pieces, axis=0)
    ratio = live[None, :] * (huber_edge / jnp.maximum(jnp.abs(weighted), huber_edge))
    qc_weight = ratio.astype(jnp.bfloat16)
    scaled = (ratio * weighted).astype(jnp.bfloat16)
    pred_wide = predictors.astype(jnp.float32)
    firsts, seconds, mirror = upper_tables(count_pred)
    pairs = (pred_wide[firsts] * pred_wide[seconds]).astype(jnp.bfloat16)
    factor = 1.0 / float(obs_dev * lax.axis_size("obs"))
    gram_terms = (
        jnp.einsum("ko,co->kc", pairs, qc_weight, preferred_element_type=jnp.float32) * factor
    )
    rhs_terms = (
        jnp.einsum("ko,co->kc", predictors, scaled, preferred_element_type=jnp.float32) * factor
    )
    gram_full, rhs_full = lax.psum((gram_terms, rhs_terms), "obs")
    width = own // lax.axis_size("obs")
    start = lax.axis_index("obs") * width
    gram_part = lax.dynamic_slice_in_dim(gram_full, start, width, 1)
    rhs_part = lax.dynamic_slice_in_dim(rhs_full, start, width, 1)
    gram_part = gram_part[mirror]
    return (gram_part, rhs_part)


def solution(mesh):
    in_specs = (P("chan", "obs"), P(None, "obs"), P(None, "chan"), P(), P("obs"))
    out_specs = (P(None, ("chan", "obs")), P(None, ("chan", "obs")))
    return jax.shard_map(
        on_device, mesh=mesh, in_specs=in_specs, out_specs=out_specs, check_vma=False
    )
```

profile of v0, /device:TPU:0, one launch (start us, length us, event | category | flops | bytes accessed | tf_op | source)
XLA Modules:
  0.0 140.2 jit_solution(5953910582028447747)
XLA Ops:
  7.2 0.0 copy-start.4
  7.2 0.0 copy-start.5
  7.2 0.0 copy-start.2
  7.2 0.0 copy-start
  7.2 0.0 copy-start.1
  7.2 0.0 all-reduce.5.cloned.1.call-start
  7.3 1.0 fusion.53
  8.3 2.4 %collective-permute-start = (bf16[31,2048]{1,0:T(8,128)(2,1)S(1)}, bf16[31,2048]{1,0:T(8,128)(2,1)S(1)}, u32[]{:S(2)}, u32[]{:S(2)}) collective-permute-start(bf16[31,2048]{1,0:T(8,128)(2,1)S(1)} %get-tuple-element.13), channel_id=1, source_target_pairs={{0,1},{1,2},{2,3},{4,5},{5,6},{6,7},{8,9},{9,10},{10,11},{12,13},{... | collective-permute-start | bytes 380936 | tf_op jit(solution)/shard_map/ppermute | solution.py:18
  10.7 1.3 collective-permute-start.1
  12.0 1.3 copy.14
  13.2 0.2 pad.9
  13.5 2.4 %reshape.95 = bf16[653312]{0:T(1024)(128)(2,1)S(1)} reshape(bf16[8,256,319]{2,1,0:T(8,128)(2,1)S(1)} %pad.9) | data formatting | bytes 2613248
  15.9 1.4 reshape.61
  17.3 9.3 %slice_reduce_fusion = (bf16[81408]{0:T(1024)(128)(2,1)S(1)}, bf16[81408]{0:T(1024)(128)(2,1)S(1)}, bf16[81408]{0:T(1024)(128)(2,1)S(1)}, bf16[81408]{0:T(1024)(...) fusion(bf16[8,81664]{1,0:T(8,128)(2,1)S(1)} %reshape.61), kind=kLoop, calls=%fused_computation.38 | loop fusion | bytes 2605056 | tf_op jit(solution)/shard_map/slice | solution.py:70
  26.6 0.0 copy-done.2
  26.6 0.1 convert_bitcast_fusion
  26.7 0.0 copy-done.4
  26.7 0.1 pad_dynamic-slice_fusion
  26.9 0.5 squeeze.24
  27.4 0.5 squeeze.25
  27.8 0.5 squeeze.26
  28.3 0.5 squeeze.27
  28.8 0.5 squeeze.28
  29.3 0.5 squeeze.29
  29.7 0.5 squeeze.30
  30.2 0.5 squeeze.31
  30.7 0.0 copy-done.1
  30.7 0.7 gather_fusion
  31.4 0.7 gather_fusion.1
  32.2 0.1 pad_dynamic-slice_fusion.15
  32.3 0.0 collective-permute-done
  32.3 2.2 %convolution_dynamic-update-slice_fusion.7 = f32[2048,2048]{1,0:T(8,128)S(1)} fusion(bf16[2048,2048]{1,0:T(8,128)(2,1)} %param.11, bf16[31,2048]{1,0:T(8,128)(2,1)S(1)} %collective-permute-done, bf16[256,318]{1,0:T(8,128)(2,1)S(1)} %squeeze.24, s32[318]{0:T(512)S(1)} %get-tuple-element.23, s32[256]{0:T(256)S(1)} %get-tuple-element.15), kind=kOutput, calls=%fused_computation.15 | convolution fusion | flops 336215040 | bytes 10777848 | tf_op jit(solution)/shard_map/dot_general | solution.py:72
  34.5 0.0 slice-start.1
  34.5 2.2 %convolution_dynamic-update-slice_fusion.6 = f32[2048,2048]{1,0:T(8,128)S(1)} fusion(f32[2048,2048]{1,0:T(8,128)S(1)} %convolution_dynamic-update-slice_fusion.7, bf16[2048,2048]{1,0:T(8,128)(2,1)} %param.11, bf16[256,318]{1,0:T(8,128)(2,1)S(1)} %squeeze.25, s32[318]{0:T(512)S(1)} %get-tuple-element.24, s32[256]{0:T(256)S(1)} %get-tuple-element.16), kind=kOutput, calls=%fused_computation.14 | convolution fusion | flops 333609984 | bytes 3607552 | tf_op jit(solution)/shard_map/dot_general | solution.py:72
  36.8 2.1 %convolution_dynamic-update-slice_fusion.5 = f32[2048,2048]{1,0:T(8,128)S(1)} fusion(f32[2048,2048]{1,0:T(8,128)S(1)} %convolution_dynamic-update-slice_fusion.6, bf16[2048,2048]{1,0:T(8,128)(2,1)} %param.11, bf16[256,318]{1,0:T(8,128)(2,1)S(1)} %squeeze.26, s32[318]{0:T(512)S(1)} %get-tuple-element.25, s32[256]{0:T(256)S(1)} %get-tuple-element.17), kind=kOutput, calls=%fused_computation.13 | convolution fusion | flops 333609984 | bytes 3607552 | tf_op jit(solution)/shard_map/dot_general | solution.py:72
  38.9 2.1 %convolution_dynamic-update-slice_fusion.4 = f32[2048,2048]{1,0:T(8,128)S(1)} fusion(f32[2048,2048]{1,0:T(8,128)S(1)} %convolution_dynamic-update-slice_fusion.5, bf16[2048,2048]{1,0:T(8,128)(2,1)} %param.11, bf16[256,318]{1,0:T(8,128)(2,1)S(1)} %squeeze.27, s32[318]{0:T(512)S(1)} %get-tuple-element.26, s32[256]{0:T(256)S(1)} %get-tuple-element.18), kind=kOutput, calls=%fused_computation.12 | convolution fusion | flops 333609984 | bytes 3607552 | tf_op jit(solution)/shard_map/dot_general | solution.py:72
  41.0 0.8 convolution_dynamic-update-slice_fusion.3
  41.8 0.8 convolution_dynamic-update-slice_fusion.2
  42.5 0.8 convolution_dynamic-update-slice_fusion.1
  43.3 0.0 collective-permute-done.1
  43.3 0.8 convolution_dynamic-update-slice_fusion
  44.1 3.9 %fusion.8 = f32[10,2048]{1,0:T(8,128)} fusion(bf16[10,2048]{1,0:T(8,128)(2,1)S(1)} %copy-done.1, f32[2048,2048]{1,0:T(8,128)S(1)} %convolution_dynamic-update-slice_fusion, f32[2048]{0:T(1024)S(1)} %convert_bitcast_fusion), kind=kOutput, calls=%fused_computation.18 | convolution fusion | flops 109072384 | bytes 16908288 | tf_op jit(solution)/shard_map/ko,co->kc/dot_general | solution.py:85
  48.0 3.8 %fusion.4 = f32[55,2048]{1,0:T(8,128)} fusion(f32[2048,2048]{1,0:T(8,128)S(1)} %convolution_dynamic-update-slice_fusion, f32[2048]{0:T(1024)S(1)} %convert_bitcast_fusion, f32[55,2048]{1,0:T(8,128)S(1)} %gather_fusion, f32[55,2048]{1,0:T(8,128)S(1)} %gather_fusion.1), kind=kOutput, calls=%fused_computation.16 | convolution fusion | flops 482682880 | bytes 18137088 | tf_op jit(solution)/shard_map/ko,co->kc/dot_general | solution.py:82
  51.8 0.0 all-reduce.5.cloned.1.call-update
  51.9 78.0 %all-reduce.5.cloned.1.call-done = (f32[55,2048]{1,0:T(8,128)}, f32[10,2048]{1,0:T(8,128)}) async-done(((f32[55,2048]{1,0:T(8,128)}, f32[10,2048]{1,0:T(8,128)}), (f32[55,2048]{1,0:T(8,128)}, f32[10,2048]{1,0:T(8,128)})) %all-reduce.5.cloned.1.call-update) | async-done | bytes 532496 | tf_op jit(solution)/shard_map/psum | solution.py:87
  129.9 0.8 constant_dynamic-slice_fusion.1
  130.7 1.3 constant_dynamic-slice_fusion
  132.0 1.3 gather_fusion.2
  (11 shorter events, 0.0 us)
Async XLA Ops:
  7.2 19.6 %copy-start.4 = (s32[55]{0:T(128)S(1)}, s32[55]{0:T(128)}, u32[]{:S(2)}) copy-start(s32[55]{0:T(128)} %constant.52) | copy-start | bytes 664
  7.2 19.5 %copy-start.5 = (s32[55]{0:T(128)S(1)}, s32[55]{0:T(128)}, u32[]{:S(2)}) copy-start(s32[55]{0:T(128)} %constant.53) | copy-start | bytes 664
  7.2 19.4 %copy-start.2 = (s32[16]{0:T(128)S(1)}, s32[16]{0:T(128)}, u32[]{:S(2)}) copy-start(s32[16]{0:T(128)} %param.15) | copy-start | bytes 196
  7.2 19.5 %copy-start = (s32[8192]{0:T(1024)S(1)}, s32[8192]{0:T(1024)}, u32[]{:S(2)}) copy-start(s32[8192]{0:T(1024)} %param.14) | copy-start | bytes 98308
  7.2 23.5 %copy-start.1 = (bf16[10,2048]{1,0:T(8,128)(2,1)S(1)}, bf16[10,2048]{1,0:T(8,128)(2,1)}, u32[]{:S(2)}) copy-start(bf16[10,2048]{1,0:T(8,128)(2,1)} %param.12) | copy-start | bytes 122884
  7.2 122.7 %all-reduce.5.cloned.1.call-start = ((), (), s32[]{:S(2)}) async-start(), calls=%async_computation | async-start | bytes 1179648 | tf_op jit(solution)/shard_map/psum | solution.py:87
  8.3 24.0 %collective-permute-start = (bf16[31,2048]{1,0:T(8,128)(2,1)S(1)}, bf16[31,2048]{1,0:T(8,128)(2,1)S(1)}, u32[]{:S(2)}, u32[]{:S(2)}) collective-permute-start(bf16[31,2048]{1,0:T(8,128)(2,1)S(1)} %get-tuple-element.13), channel_id=1, source_target_pairs={{0,1},{1,2},{2,3},{4,5},{5,6},{6,7},{8,9},{9,10},{10,11},{12,13},{... | collective-permute-start | bytes 380936 | tf_op jit(solution)/shard_map/ppermute | solution.py:18
  10.7 32.6 %collective-permute-start.1 = (bf16[31,2048]{1,0:T(8,128)(2,1)S(1)}, bf16[31,2048]{1,0:T(8,128)(2,1)S(1)}, u32[]{:S(2)}, u32[]{:S(2)}) collective-permute-start(bf16[31,2048]{1,0:T(8,128)(2,1)S(1)} %get-tuple-element.12), channel_id=1, source_target_pairs={{1,0},{2,1},{3,2},{5,4},{6,5},{7,6},{9,8},{10,9},{11,10},{13,12},{... | collective-permute-start | bytes 380936 | tf_op jit(solution)/shard_map/ppermute | solution.py:20
  32.3 8.7 %slice-start = ((s8[8388608]{0:T(1024)(128)(4,1)}), s8[4194304]{0:T(1024)(128)(4,1)S(1)}, s32[]{:S(2)}) async-start(s8[8388608]{0:T(1024)(128)(4,1)} %bitcast.7), calls=%async_computation.1 | async-start | bytes 8388608
  34.5 6.5 %slice-start.1 = ((s8[8388608]{0:T(1024)(128)(4,1)}), s8[4194304]{0:T(1024)(128)(4,1)S(1)}, s32[]{:S(2)}) async-start(s8[8388608]{0:T(1024)(128)(4,1)} %bitcast.7), calls=%async_computation.2 | async-start | bytes 8388608
  48.0 3.9 %copy-start.3 = (s32[100]{0:T(128)S(1)}, s32[100]{0:T(128)}, u32[]{:S(2)}) copy-start(s32[100]{0:T(128)} %constant.54) | copy-start | bytes 1204
Sparse Core Ops, SparseCore 0:
  52.0 77.8 all-reduce.4
where the time goes:
time: 141 us; the launch traced here: 140 us
  waiting for transfers between devices  78 us (55%)
  local copies, waits for them, and re-layouts  24.6 us (17%)
  matrix products  19.4 us (14%)
  between operations  14.3 us (10%)
  starting transfers between devices  3.73 us (3%)
    psum x1, waiting for transfers between devices, on_device(): gram_full, rhs_full = lax.psum((gram_terms, rhs_terms), 'obs')  78 us
    dot_general x8, matrix products, on_device(): pieces.append(jnp.dot(matrix, window, preferred_element_type=jnp.float32))  11.7 us
    slice x1, local copies, waits for them, and re-layouts, on_device(): matrix = jnp.where(same, skewed[number], jnp.zeros_like(skewed[number]))  9.3 us
    dot_general x1, matrix products, on_device(): jnp.einsum('ko,co->kc', predictors, scaled, preferred_element_type=jnp.fl...  3.88 us
    dot_general x1, matrix products, on_device(): jnp.einsum('ko,co->kc', pairs, qc_weight, preferred_element_type=jnp.floa...  3.85 us
    squeeze x8, local copies, waits for them, and re-layouts, on_device(): matrix = jnp.where(same, skewed[number], jnp.zeros_like(skewed[number]))  3.75 us
  transfers between devices with their start and end apart: 3, of which 1 were waited for; matrix products, arithmetic and copies ran while one was open for 22% of the time, Pallas kernels for 0%

commit v1 on v0

v1 whole, which is shorter than its diff:
```python
import functools

import jax
import jax.numpy as jnp
import numpy as np
from jax import lax
from jax.experimental import pallas as pl
from jax.experimental.pallas import tpu as pltpu
from jax.sharding import PartitionSpec as P

huber_edge = 1.0
LANES = 128
HALO = 32
TILE = 128
OBS_CHUNK = 512
MESH = pl.DeviceIdType.MESH


def mirror_rows(count):
    rows = []
    for first in range(count):
        for second in range(count):
            low = min(first, second)
            high = max(first, second)
            rows.append(low * count - low * (low - 1) // 2 + high - low)
    return rows


def peer(axis, index):
    if axis == "obs":
        return (index, lax.axis_index("chan"))
    return (lax.axis_index("obs"), index)


def kernel(
    n_obs,
    n_chan,
    scatter,
    dep,
    pred,
    inv,
    ids_win,
    ids_own,
    counts,
    *rest,
):
    if scatter:
        gram_out, rhs_out = rest[:2]
        rest = rest[2:]
    else:
        part_out = rest[0]
        rest = rest[1:]
    (
        window,
        wide,
        table_q,
        table_s,
        flip,
        stage,
        landed,
        total,
        load_sem,
        halo_send,
        halo_recv,
        part_send,
        part_recv,
    ) = rest
    own, obs_dev = dep.shape
    preds = pred.shape[0]
    offsets = inv.shape[0]
    half = offsets // 2
    upper = preds * (preds + 1) // 2
    rows = stage.shape[1]
    blocks = stage.shape[0]
    width = own // blocks
    lines = counts.shape[0]
    slots = obs_dev // lines
    me = lax.axis_index("obs")
    chan = lax.axis_index("chan")
    right = lax.rem(chan + 1, n_chan)
    left = lax.rem(chan + n_chan - 1, n_chan)

    barrier = pltpu.get_barrier_semaphore()
    for index in (left, right):
        pl.semaphore_signal(barrier, inc=1, device_id=peer("chan", index), device_id_type=MESH)
    greeted = 2
    if scatter:
        for step in range(1, n_obs):
            index = lax.rem(me + step, n_obs)
            pl.semaphore_signal(barrier, inc=1, device_id=peer("obs", index), device_id_type=MESH)
        greeted += n_obs - 1

    here = lax.rem(me, blocks)
    stride = jnp.where(here < blocks // 2, 1, blocks - 1)

    def block_at(place):
        return lax.rem(here + stride * place, blocks)

    def load(place):
        start = pl.multiple_of(block_at(place) * width, width)
        return pltpu.make_async_copy(
            dep.at[pl.ds(start, width), :],
            window.at[pl.ds(start + HALO, width), :],
            load_sem.at[place],
        )

    def start_load(place, carry):
        load(place).start()
        return carry

    lax.fori_loop(0, blocks, start_load, 0)

    values = pred[...].astype(jnp.float32)
    wide[...] = jnp.zeros_like(wide)
    first_row = 0
    for first in range(preds):
        count = preds - first
        wide[first_row : first_row + count, :] = values[first:, :] * values[first : first + 1, :]
        first_row += count
    wide[upper : upper + preds, :] = values
    lane = lax.broadcasted_iota(jnp.int32, (slots, LANES), 1)

    def turn(line, carry):
        at = pl.ds(pl.multiple_of(line * slots, slots), slots)
        slot = lax.broadcasted_iota(jnp.int32, (LANES, slots), 1)
        live = jnp.where(slot < counts[line], wide[:, at], 0.0)
        turned = live.T
        table_q[at, :] = jnp.where(lane < upper, turned, 0.0).astype(jnp.bfloat16)
        table_s[at, :] = jnp.where(lane >= upper, turned, 0.0).astype(jnp.bfloat16)
        return carry

    lax.fori_loop(0, lines, turn, 0)
    flip[...] = jnp.zeros_like(flip)

    pl.semaphore_wait(barrier, greeted)
    to_left = pltpu.make_async_remote_copy(
        src_ref=dep.at[pl.ds(0, HALO), :],
        dst_ref=window.at[pl.ds(own + HALO, HALO), :],
        send_sem=halo_send.at[0],
        recv_sem=halo_recv.at[0],
        device_id=peer("chan", left),
        device_id_type=MESH,
    )
    to_right = pltpu.make_async_remote_copy(
        src_ref=dep.at[pl.ds(own - HALO, HALO), :],
        dst_ref=window.at[pl.ds(0, HALO), :],
        send_sem=halo_send.at[1],
        recv_sem=halo_recv.at[1],
        device_id=peer("chan", right),
        device_id_type=MESH,
    )
    to_left.start()
    to_right.start()

    def send_part(step):
        return pltpu.make_async_remote_copy(
            src_ref=stage.at[step],
            dst_ref=landed.at[me],
            send_sem=part_send.at[step],
            recv_sem=part_recv.at[me],
            device_id=peer("obs", block_at(step + 1)),
            device_id_type=MESH,
        )

    def arrived(sender):
        return pltpu.make_async_remote_copy(
            src_ref=stage.at[0],
            dst_ref=landed.at[sender],
            send_sem=part_send.at[0],
            recv_sem=part_recv.at[sender],
            device_id=peer("obs", sender),
            device_id_type=MESH,
        )

    load(0).wait()
    load(1).wait()

    def one_block(step, carry):
        block = block_at(step + 1)

        @pl.when(step + 2 < blocks)
        def _():
            load(step + 2).wait()

        @pl.when(block == blocks - 1)
        def _():
            to_left.wait_recv()

        @pl.when(block == 0)
        def _():
            to_right.wait_recv()

        for part in range(width // TILE):
            first = pl.multiple_of(block * width + part * TILE, TILE)
            flip[0:offsets, :] = inv[:, pl.ds(first, TILE)].astype(jnp.float32)
            flip[64:65, :] = ids_own[:, pl.ds(first, TILE)]
            turned = flip[...].T
            own_id = turned[:, 64:65]
            place = lax.broadcasted_iota(jnp.int32, turned.shape, 1)
            turned = jnp.where(place < offsets, turned, 0.0)
            skewed = pltpu.roll(
                jnp.concatenate([turned, jnp.zeros_like(turned)], axis=1),
                HALO - half,
                1,
                stride=1,
                stride_axis=0,
            )
            same = ids_win[:, pl.ds(first, 2 * TILE)] == own_id
            matrix = jnp.where(same, skewed, 0.0).astype(jnp.bfloat16)
            matrix = matrix[:, : TILE + 2 * HALO]
            sums = jnp.zeros((TILE, LANES), jnp.float32)
            for at in range(0, obs_dev, OBS_CHUNK):
                weighted = jnp.dot(
                    matrix,
                    window[pl.ds(first, TILE + 2 * HALO), at : at + OBS_CHUNK],
                    preferred_element_type=jnp.float32,
                )
                ratio = huber_edge / jnp.maximum(jnp.abs(weighted), huber_edge)
                qc_weight = ratio.astype(jnp.bfloat16)
                scaled = jnp.clip(weighted, -huber_edge, huber_edge).astype(jnp.bfloat16)
                sums += jnp.dot(
                    qc_weight,
                    table_q[at : at + OBS_CHUNK, :],
                    preferred_element_type=jnp.float32,
                )
                sums += jnp.dot(
                    scaled,
                    table_s[at : at + OBS_CHUNK, :],
                    preferred_element_type=jnp.float32,
                )
            result = sums.T[:rows, :]
            if scatter:
                stage[step, :, part * TILE : (part + 1) * TILE] = result
            else:
                part_out[:, pl.ds(first, TILE)] = result

        if scatter:

            @pl.when(step < blocks - 1)
            def _():
                send_part(step).start()

        return carry

    lax.fori_loop(0, blocks, one_block, 0)
    to_left.wait_send()
    to_right.wait_send()

    if scatter:
        total[...] = stage[blocks - 1]

        def gather(step, carry):
            sender = block_at(blocks - step)
            arrived(sender).wait_recv()
            total[...] += landed[sender]
            return carry

        lax.fori_loop(1, blocks, gather, 0)
        factor = 1.0 / float(obs_dev * n_obs)
        total[...] = total[...] * factor
        for row, source in enumerate(mirror_rows(preds)):
            gram_out[row : row + 1, :] = total[source : source + 1, :]
        rhs_out[...] = total[upper : upper + preds, :]

        def drain(step, carry):
            send_part(step).wait_send()
            return carry

        lax.fori_loop(0, blocks - 1, drain, 0)


def on_device(departures, predictors, inv_band, band_id, line_counts):
    own, obs_dev = departures.shape
    preds = predictors.shape[0]
    upper = preds * (preds + 1) // 2
    n_obs = lax.axis_size("obs")
    n_chan = lax.axis_size("chan")
    share = own // n_obs
    scatter = share % TILE == 0
    blocks = n_obs if scatter else own // (2 * TILE)
    width = own // blocks
    rows = -(-(upper + preds) // 8) * 8
    base = lax.axis_index("chan") * own
    marked = jnp.pad(band_id, (HALO, TILE), constant_values=-1).astype(jnp.float32)
    ids_win = lax.dynamic_slice_in_dim(marked, base, own + TILE)[None, :]
    ids_own = lax.dynamic_slice_in_dim(marked, base + HALO, own)[None, :]
    if scatter:
        out_shape = (
            jax.ShapeDtypeStruct((preds * preds, share), jnp.float32),
            jax.ShapeDtypeStruct((preds, share), jnp.float32),
        )
    else:
        out_shape = (jax.ShapeDtypeStruct((rows, own), jnp.float32),)
    vmem = pl.BlockSpec(memory_space=pltpu.VMEM)
    landing = (n_obs, rows, width) if scatter else (1, 8, LANES)
    outs = pl.pallas_call(
        functools.partial(kernel, n_obs, n_chan, scatter),
        out_shape=out_shape,
        in_specs=[
            pl.BlockSpec(memory_space=pl.ANY),
            vmem,
            vmem,
            vmem,
            vmem,
            pl.BlockSpec(memory_space=pltpu.SMEM),
        ],
        out_specs=tuple(vmem for _ in out_shape),
        scratch_shapes=[
            pltpu.VMEM((own + 2 * HALO, obs_dev), jnp.bfloat16),
            pltpu.VMEM((LANES, obs_dev), jnp.float32),
            pltpu.VMEM((obs_dev, LANES), jnp.bfloat16),
            pltpu.VMEM((obs_dev, LANES), jnp.bfloat16),
            pltpu.VMEM((LANES, TILE), jnp.float32),
            pltpu.VMEM((blocks, rows, width), jnp.float32),
            pltpu.VMEM(landing, jnp.float32),
            pltpu.VMEM((rows, width), jnp.float32),
            pltpu.SemaphoreType.DMA((blocks,)),
            pltpu.SemaphoreType.DMA((2,)),
            pltpu.SemaphoreType.DMA((2,)),
            pltpu.SemaphoreType.DMA((blocks,)),
            pltpu.SemaphoreType.DMA((n_obs,)),
        ],
        compiler_params=pltpu.CompilerParams(
            collective_id=0,
            has_side_effects=True,
            vmem_limit_bytes=40 * 1024 * 1024,
        ),
        name="normal_equations",
    )(departures, predictors, inv_band, ids_win, ids_own, line_counts)
    if scatter:
        return outs[0], outs[1]
    factor = 1.0 / float(obs_dev * n_obs)
    part = lax.psum_scatter(outs[0], "obs", scatter_dimension=1, tiled=True) * factor
    mirror = np.array(mirror_rows(preds))
    return part[mirror], part[upper : upper + preds]


def solution(mesh):
    in_specs = (P("chan", "obs"), P(None, "obs"), P(None, "chan"), P(), P("obs"))
    out_specs = (P(None, ("chan", "obs")), P(None, ("chan", "obs")))
    return jax.shard_map(
        on_device, mesh=mesh, in_specs=in_specs, out_specs=out_specs, check_vma=False
    )
```

time: 141 us -> 36.3 us (0.26)
  waiting for transfers between devices: 78 us -> 0 us
  Pallas kernels: 0 us -> 27.3 us
  matrix products: 19.4 us -> 0 us
  local copies, waits for them, and re-layouts: 24.6 us -> 7.23 us
  between operations: 14.3 us -> 0.66 us
  starting transfers between devices: 3.73 us -> 0 us
    psum x1 -> x0, waiting for transfers between devices: 78 us -> none  [on_device(): gram_full, rhs_full = lax.psum((gram_terms, rhs_terms), 'obs')]
    pallas_call x0 -> x1, Pallas kernels: none -> 27.3 us  [on_device(): pl.pallas_call(functools.partial(kernel, n_obs, n_chan, scatter), out_sha...]
    dot_general x10 -> x0, matrix products: 19.4 us -> none  [the longest x8 11.7 us: on_device(): pieces.append(jnp.dot(matrix, window, preferred_element_type=jnp.float32))]
    slice x4 -> x0, local copies, waits for them, and re-layouts: 10.6 us -> none  [the longest x1 9.3 us: on_device(): matrix = jnp.where(same, skewed[number], jnp.zeros_like(skewed[number]))]
    unnamed x17 -> x10, local copies, waits for them, and re-layouts: 2.48 us -> 7.07 us
    squeeze x8 -> x0, local copies, waits for them, and re-layouts: 3.75 us -> none  [on_device(): matrix = jnp.where(same, skewed[number], jnp.zeros_like(skewed[number]))]
    ppermute x2 -> x0, starting transfers between devices: 3.7 us -> none  [the longest x1 2.4 us: with_halo(): lax.ppermute(tail, axis, [(i, (i + 1) % count) for i in range(ends)])]
    gather x3 -> x0, local copies, waits for them, and re-layouts: 2.8 us -> none  [the longest x2 1.46 us: on_device(): pairs = (pred_wide[firsts] * pred_wide[seconds]).astype(jnp.bfloat16)]
  transfers between devices with their start and end apart: 3 -> 0, of which waited for: 1 -> 0; matrix products, arithmetic and copies ran while one was open for 22% -> 0% of each run, Pallas kernels for 0% -> 0%
where the time goes in v1:
time: 36.3 us; the launch traced here: 36 us
  Pallas kernels  27.3 us (75%)
  local copies, waits for them, and re-layouts  7.23 us (20%)
  other arithmetic  0.84 us (2%)
  between operations  0.66 us (2%)
    pallas_call x1, Pallas kernels, on_device(): pl.pallas_call(functools.partial(kernel, n_obs, n_chan, scatter), out_sha...  27.3 us
    unnamed x10, local copies, waits for them, and re-layouts  7.07 us
    convert_element_type x1, other arithmetic, on_device(): jnp.pad(band_id, (HALO, TILE), constant_values=-1).astype(jnp.float32)  0.84 us

profile of v1, /device:TPU:0, one launch (start us, length us, event | category | flops | bytes accessed | tf_op | source)
XLA Modules:
  0.0 36.0 jit_solution(13430321106976082132)
XLA Ops:
  0.6 0.8 %pad_convert_fusion = f32[8352]{0:T(1024)S(1)} fusion(s32[8192]{0:T(1024)} %param.8), kind=kLoop, calls=%fused_computation | loop fusion | flops 8352 | bytes 66176 | tf_op jit(solution)/shard_map/convert_element_type | solution.py:284
  1.5 0.1 dynamic_slice.7
  1.5 0.1 dynamic_slice.6
  1.6 0.0 copy-start
  1.7 3.4 %copy-done = bf16[2048,2048]{1,0:T(8,128)(2,1)S(1)} copy-done((bf16[2048,2048]{1,0:T(8,128)(2,1)S(1)}, bf16[2048,2048]{1,0:T(8,128)(2,1)}, u32[]{:S(2)}) %copy-start) | copy-done | bytes 8388632
  5.0 0.0 copy-start.1
  5.0 0.9 %copy-done.1 = bf16[63,2048]{1,0:T(8,128)(2,1)S(1)} copy-done((bf16[63,2048]{1,0:T(8,128)(2,1)S(1)}, bf16[63,2048]{1,0:T(8,128)(2,1)}, u32[]{:S(2)}) %copy-start.1) | copy-done | bytes 258072
  6.0 0.0 copy-start.2
  6.0 0.8 %copy-done.2 = bf16[10,2048]{1,0:T(8,128)(2,1)S(1)} copy-done((bf16[10,2048]{1,0:T(8,128)(2,1)S(1)}, bf16[10,2048]{1,0:T(8,128)(2,1)}, u32[]{:S(2)}) %copy-start.2) | copy-done | bytes 40984
  6.8 0.0 copy-start.3
  6.8 0.7 %copy-done.3 = s32[16]{0:T(128)S(1)} copy-done((s32[16]{0:T(128)S(1)}, s32[16]{0:T(128)}, u32[]{:S(2)}) %copy-start.3) | copy-done | bytes 88
  7.5 27.3 %normal_equations.1 = (f32[100,256]{1,0:T(8,128)S(1)}, f32[10,256]{1,0:T(8,128)S(1)}) custom-call(bf16[2048,2048]{1,0:T(8,128)(2,1)S(1)} %copy-done, bf16[10,2048]{1,0:T(8,128)(2,1)S(1)} %copy-done.2, bf16[63,2048]{1,0:T(8,128)(2,1)S(1)} %copy-done.1, f32[1,2176]{1,0:T(1,128)S(1)} %broadcast_in_dim.6.ids_win, f32[1,2048]{1,0:T(1,128)S(1)} %bitcast.1, ...), custom_call_target="tpu_custom_call" | custom-call | tf_op jit(solution)/shard_map/normal_equations/pallas_call | solution.py:296
  34.8 0.6 %copy.9 = f32[100,256]{1,0:T(8,128)} copy(f32[100,256]{1,0:T(8,128)S(1)} %get-tuple-element.4) | data formatting | bytes 204800
  35.4 0.6 %copy.10 = f32[10,256]{1,0:T(8,128)} copy(f32[10,256]{1,0:T(8,128)S(1)} %get-tuple-element.5) | data formatting | bytes 20480
  (1 shorter events, 0.0 us)
Async XLA Ops:
  1.6 3.4 %copy-start = (bf16[2048,2048]{1,0:T(8,128)(2,1)S(1)}, bf16[2048,2048]{1,0:T(8,128)(2,1)}, u32[]{:S(2)}) copy-start(bf16[2048,2048]{1,0:T(8,128)(2,1)} %dep.1) | copy-start | bytes 25165828
  5.0 0.9 %copy-start.1 = (bf16[63,2048]{1,0:T(8,128)(2,1)S(1)}, bf16[63,2048]{1,0:T(8,128)(2,1)}, u32[]{:S(2)}) copy-start(bf16[63,2048]{1,0:T(8,128)(2,1)} %inv.1) | copy-start | bytes 774148
  6.0 0.8 %copy-start.2 = (bf16[10,2048]{1,0:T(8,128)(2,1)S(1)}, bf16[10,2048]{1,0:T(8,128)(2,1)}, u32[]{:S(2)}) copy-start(bf16[10,2048]{1,0:T(8,128)(2,1)} %pred_.1) | copy-start | bytes 122884
  6.8 0.7 %copy-start.3 = (s32[16]{0:T(128)S(1)}, s32[16]{0:T(128)}, u32[]{:S(2)}) copy-start(s32[16]{0:T(128)} %counts.1) | copy-start | bytes 196

commit v2 on v1

v2 whole, which is shorter than its diff:
```python
import functools

import jax
import jax.numpy as jnp
import numpy as np
from jax import lax
from jax.experimental import pallas as pl
from jax.experimental.pallas import tpu as pltpu
from jax.sharding import PartitionSpec as P

huber_edge = 1.0
LANES = 128
HALO = 32
TILE = 128
OBS_CHUNK = 512
MESH = pl.DeviceIdType.MESH


def mirror_rows(count):
    rows = []
    for first in range(count):
        for second in range(count):
            low = min(first, second)
            high = max(first, second)
            rows.append(low * count - low * (low - 1) // 2 + high - low)
    return rows


def peer(axis, index):
    if axis == "obs":
        return (index, lax.axis_index("chan"))
    return (lax.axis_index("obs"), index)


def kernel(n_obs, n_chan, scatter, dep, pred, inv, ids, counts, *rest):
    if scatter:
        gram_out, rhs_out = rest[:2]
        rest = rest[2:]
    else:
        part_out = rest[0]
        rest = rest[1:]
    (
        window,
        pred_in,
        inv_in,
        ids_in,
        counts_in,
        wide,
        table,
        flip,
        bands,
        stage,
        landed_x,
        landed_z,
        total,
        small_sem,
        load_sem,
        halo_send,
        halo_recv,
        x_send,
        x_recv,
        z_send,
        z_recv,
    ) = rest
    own, obs_dev = dep.shape
    preds = pred.shape[0]
    offsets = inv.shape[0]
    half = offsets // 2
    upper = preds * (preds + 1) // 2
    blocks, rows, width = stage.shape
    tiles = width // TILE
    pairs = blocks // 2
    lines = counts.shape[0]
    slots = obs_dev // lines
    me = lax.axis_index("obs")
    chan = lax.axis_index("chan")
    right = lax.rem(chan + 1, n_chan)
    left = lax.rem(chan + n_chan - 1, n_chan)
    spot = lax.rem(me, blocks)
    col = lax.rem(spot, 2)
    lev = lax.div(spot, 2)
    stride = jnp.where(lev < pairs // 2, 1, pairs - 1)

    def level_at(turn):
        return lax.rem(lev + stride * (turn + 1), pairs)

    def block_at(step):
        side = jnp.where(step < pairs, 1 - col, col)
        return 2 * level_at(lax.rem(step, pairs)) + side

    barrier = pltpu.get_barrier_semaphore()
    for index in (left, right):
        pl.semaphore_signal(barrier, inc=1, device_id=peer("chan", index), device_id_type=MESH)
    greeted = 2
    if scatter:
        partner = me + 1 - 2 * col
        pl.semaphore_signal(barrier, inc=1, device_id=peer("obs", partner), device_id_type=MESH)
        for turn in range(pairs - 1):
            index = 2 * level_at(turn) + col
            pl.semaphore_signal(barrier, inc=1, device_id=peer("obs", index), device_id_type=MESH)
        greeted += pairs

    base = pl.multiple_of(chan * own, own)
    smalls = [
        pltpu.make_async_copy(pred, pred_in, small_sem.at[0]),
        pltpu.make_async_copy(counts, counts_in, small_sem.at[1]),
        pltpu.make_async_copy(inv, inv_in, small_sem.at[2]),
        pltpu.make_async_copy(
            ids.at[:, pl.ds(base, own)], ids_in.at[:, pl.ds(LANES, own)], small_sem.at[3]
        ),
    ]
    before = pltpu.make_async_copy(
        ids.at[:, pl.ds(pl.multiple_of(jnp.maximum(base - LANES, 0), LANES), LANES)],
        ids_in.at[:, pl.ds(0, LANES)],
        small_sem.at[4],
    )
    after = pltpu.make_async_copy(
        ids.at[:, pl.ds(pl.multiple_of(jnp.minimum(base + own, own * n_chan - LANES), LANES), LANES)],
        ids_in.at[:, pl.ds(LANES + own, LANES)],
        small_sem.at[5],
    )
    for copy in smalls:
        copy.start()
    before.start()
    after.start()

    origin = block_at(0) + blocks - jnp.where(stride == 1, 1, blocks - 1)
    hop = jnp.where(stride == 1, 1, blocks - 1)

    def load(place):
        chunk = lax.rem(origin + hop * place, blocks)
        start = pl.multiple_of(chunk * width, width)
        return pltpu.make_async_copy(
            dep.at[pl.ds(start, width), :],
            window.at[pl.ds(start + HALO, width), :],
            load_sem.at[place],
        )

    def start_load(place, carry):
        load(place).start()
        return carry

    lax.fori_loop(0, blocks, start_load, 0)

    smalls[0].wait()
    smalls[1].wait()
    values = pred_in[...].astype(jnp.float32)
    wide[upper + preds :, :] = jnp.zeros((LANES - upper - preds, obs_dev), jnp.float32)
    first_row = 0
    for first in range(preds):
        count = preds - first
        wide[first_row : first_row + count, :] = values[first:, :] * values[first : first + 1, :]
        first_row += count
    wide[upper : upper + preds, :] = values
    lane = lax.broadcasted_iota(jnp.int32, (slots, LANES), 1)

    def turn_line(line, carry):
        at = pl.ds(pl.multiple_of(line * slots, slots), slots)
        slot = lax.broadcasted_iota(jnp.int32, (LANES, slots), 1)
        live = jnp.where(slot < counts_in[line], wide[:, at], 0.0)
        turned = live.T
        per = OBS_CHUNK // slots
        spot_q = pl.multiple_of(lax.div(line, per) * 2 * OBS_CHUNK + lax.rem(line, per) * slots, slots)
        table[pl.ds(spot_q, slots), :] = jnp.where(lane < upper, turned, 0.0).astype(jnp.bfloat16)
        table[pl.ds(spot_q + OBS_CHUNK, slots), :] = jnp.where(lane >= upper, turned, 0.0).astype(
            jnp.bfloat16
        )
        return carry

    lax.fori_loop(0, lines, turn_line, 0, unroll=2)

    pl.semaphore_wait(barrier, greeted)
    to_left = pltpu.make_async_remote_copy(
        src_ref=dep.at[pl.ds(0, HALO), :],
        dst_ref=window.at[pl.ds(own + HALO, HALO), :],
        send_sem=halo_send.at[0],
        recv_sem=halo_recv.at[0],
        device_id=peer("chan", left),
        device_id_type=MESH,
    )
    to_right = pltpu.make_async_remote_copy(
        src_ref=dep.at[pl.ds(own - HALO, HALO), :],
        dst_ref=window.at[pl.ds(0, HALO), :],
        send_sem=halo_send.at[1],
        recv_sem=halo_recv.at[1],
        device_id=peer("chan", right),
        device_id_type=MESH,
    )
    to_left.start()
    to_right.start()

    smalls[2].wait()
    smalls[3].wait()
    before.wait()
    after.wait()

    @pl.when(chan == 0)
    def _():
        ids_in[:, 0:LANES] = jnp.full((1, LANES), -1, jnp.int32)

    @pl.when(chan == n_chan - 1)
    def _():
        ids_in[:, LANES + own :] = jnp.full((1, LANES), -1, jnp.int32)

    flip[...] = jnp.zeros_like(flip)

    def build(group, carry):
        for lane_of in range(flip.shape[0]):
            first = pl.multiple_of((group * flip.shape[0] + lane_of) * TILE, TILE)
            near = ids_in[:, pl.ds(first, 3 * TILE)].astype(jnp.float32)
            flip[lane_of, 0:offsets, :] = inv_in[:, pl.ds(first, TILE)].astype(jnp.float32)
            flip[lane_of, 64:65, :] = near[:, TILE : 2 * TILE]
            turned = flip[lane_of].T
            own_id = turned[:, 64:65]
            place = lax.broadcasted_iota(jnp.int32, turned.shape, 1)
            turned = jnp.where(place < offsets, turned, 0.0)
            skewed = pltpu.roll(
                jnp.concatenate([turned, jnp.zeros_like(turned)], axis=1),
                HALO - half,
                1,
                stride=1,
                stride_axis=0,
            )
            same = near[:, TILE - HALO : 3 * TILE - HALO] == own_id
            bands[pl.ds(first, TILE), :] = jnp.where(same, skewed, 0.0).astype(jnp.bfloat16)
        return carry

    lax.fori_loop(0, own // TILE // flip.shape[0], build, 0)

    def send_x(turn):
        return pltpu.make_async_remote_copy(
            src_ref=stage.at[turn],
            dst_ref=landed_x.at[turn],
            send_sem=x_send.at[turn],
            recv_sem=x_recv.at[turn],
            device_id=peer("obs", partner),
            device_id_type=MESH,
        )

    def send_z(turn):
        return pltpu.make_async_remote_copy(
            src_ref=stage.at[pairs + turn],
            dst_ref=landed_z.at[lev],
            send_sem=z_send.at[turn],
            recv_sem=z_recv.at[lev],
            device_id=peer("obs", 2 * level_at(turn) + col),
            device_id_type=MESH,
        )

    def from_z(turn):
        sender = level_at(turn)
        return pltpu.make_async_remote_copy(
            src_ref=stage.at[pairs],
            dst_ref=landed_z.at[sender],
            send_sem=z_send.at[0],
            recv_sem=z_recv.at[sender],
            device_id=peer("obs", 2 * sender + col),
            device_id_type=MESH,
        )

    load(0).wait()

    def one_block(step, carry):
        block = block_at(step)

        @pl.when(step < pairs)
        def _():
            load(2 * step + 1).wait()

        @pl.when(step < pairs - 1)
        def _():
            load(2 * step + 2).wait()

        @pl.when(block == blocks - 1)
        def _():
            to_left.wait_recv()

        @pl.when(block == 0)
        def _():
            to_right.wait_recv()

        start = pl.multiple_of(block * width, width)
        extent = TILE + 2 * HALO
        sums = jnp.zeros((width, LANES), jnp.float32)
        for at in range(0, obs_dev, OBS_CHUNK):
            parts = []
            for part in range(tiles):
                first = pl.multiple_of(start + part * TILE, TILE)
                weighted = jnp.dot(
                    bands[pl.ds(first, TILE), 0:extent],
                    window[pl.ds(first, extent), at : at + OBS_CHUNK],
                    preferred_element_type=jnp.float32,
                )
                ratio = huber_edge / jnp.maximum(jnp.abs(weighted), huber_edge)
                qc_weight = ratio.astype(jnp.bfloat16)
                scaled = jnp.clip(weighted, -huber_edge, huber_edge).astype(jnp.bfloat16)
                parts.append(jnp.concatenate([qc_weight, scaled], axis=1))
            sums += jnp.dot(
                jnp.concatenate(parts, axis=0),
                table[2 * at : 2 * (at + OBS_CHUNK), :],
                preferred_element_type=jnp.float32,
            )
        result = sums.T[:rows, :]
        if not scatter:
            part_out[:, pl.ds(start, width)] = result
            return carry
        turn = lax.rem(step, pairs)

        @pl.when(step < pairs)
        def _():
            stage[step] = result
            send_x(turn).start()

        @pl.when(step >= pairs)
        def _():
            send_x(turn).wait_recv()
            stage[step] = result + landed_x[turn]

            @pl.when(step < blocks - 1)
            def _():
                send_z(turn).start()

        return carry

    lax.fori_loop(0, blocks, one_block, 0)
    to_left.wait_send()
    to_right.wait_send()

    if scatter:
        sums = stage[blocks - 1]
        for turn in range(pairs - 2, -1, -1):
            from_z(turn).wait_recv()
            sums = sums + landed_z[level_at(turn)]
        total[...] = sums * (1.0 / float(obs_dev * n_obs))
        for row, source in enumerate(mirror_rows(preds)):
            gram_out[row : row + 1, :] = total[source : source + 1, :]
        rhs_out[...] = total[upper : upper + preds, :]
        for turn in range(pairs):
            send_x(turn).wait_send()
        for turn in range(pairs - 1):
            send_z(turn).wait_send()


def on_device(departures, predictors, inv_band, band_id, line_counts):
    own, obs_dev = departures.shape
    preds = predictors.shape[0]
    upper = preds * (preds + 1) // 2
    n_obs = lax.axis_size("obs")
    n_chan = lax.axis_size("chan")
    share = own // n_obs
    scatter = share % TILE == 0 and n_obs % 2 == 0
    blocks = n_obs if scatter else own // (2 * TILE)
    width = own // blocks
    rows = -(-(upper + preds) // 8) * 8
    if scatter:
        out_shape = (
            jax.ShapeDtypeStruct((preds * preds, share), jnp.float32),
            jax.ShapeDtypeStruct((preds, share), jnp.float32),
        )
    else:
        out_shape = (jax.ShapeDtypeStruct((rows, own), jnp.float32),)
    vmem = pl.BlockSpec(memory_space=pltpu.VMEM)
    hbm = pl.BlockSpec(memory_space=pltpu.HBM)
    pairs = blocks // 2
    landing = (pairs, rows, width) if scatter else (1, 8, LANES)
    dma = pltpu.SemaphoreType.DMA
    outs = pl.pallas_call(
        functools.partial(kernel, n_obs, n_chan, scatter),
        out_shape=out_shape,
        in_specs=[hbm] * 5,
        out_specs=tuple(vmem for _ in out_shape),
        scratch_shapes=[
            pltpu.VMEM((own + 2 * HALO, obs_dev), jnp.bfloat16),
            pltpu.VMEM(predictors.shape, jnp.bfloat16),
            pltpu.VMEM(inv_band.shape, jnp.bfloat16),
            pltpu.VMEM((1, own + 2 * LANES), jnp.int32),
            pltpu.SMEM(line_counts.shape, jnp.int32),
            pltpu.VMEM((LANES, obs_dev), jnp.float32),
            pltpu.VMEM((2 * obs_dev, LANES), jnp.bfloat16),
            pltpu.VMEM((4, LANES, TILE), jnp.float32),
            pltpu.VMEM((own, 2 * TILE), jnp.bfloat16),
            pltpu.VMEM((blocks, rows, width), jnp.float32),
            pltpu.VMEM(landing, jnp.float32),
            pltpu.VMEM(landing, jnp.float32),
            pltpu.VMEM((rows, width), jnp.float32),
            dma((6,)),
            dma((blocks,)),
            dma((2,)),
            dma((2,)),
            dma((pairs,)),
            dma((pairs,)),
            dma((pairs,)),
            dma((pairs,)),
        ],
        compiler_params=pltpu.CompilerParams(
            collective_id=0,
            has_side_effects=True,
            vmem_limit_bytes=67043328,
        ),
        name="normal_equations",
    )(departures, predictors, inv_band, band_id[None, :], line_counts)
    if scatter:
        return outs[0], outs[1]
    factor = 1.0 / float(obs_dev * n_obs)
    part = lax.psum_scatter(outs[0], "obs", scatter_dimension=1, tiled=True) * factor
    mirror = np.array(mirror_rows(preds))
    return part[mirror], part[upper : upper + preds]


def solution(mesh):
    in_specs = (P("chan", "obs"), P(None, "obs"), P(None, "chan"), P(), P("obs"))
    out_specs = (P(None, ("chan", "obs")), P(None, ("chan", "obs")))
    return jax.shard_map(
        on_device, mesh=mesh, in_specs=in_specs, out_specs=out_specs, check_vma=False
    )
```

time: 36.3 us -> 28.3 us (0.78)
  local copies, waits for them, and re-layouts: 7.23 us -> 2.87 us
  Pallas kernels: 27.3 us -> 24.6 us
  other arithmetic: 0.84 us -> 0 us
    unnamed x10 -> x2, local copies, waits for them, and re-layouts: 7.07 us -> 2.87 us
    pallas_call x1, Pallas kernels: 27.3 us -> 24.6 us  [on_device(): pl.pallas_call(functools.partial(kernel, n_obs, n_chan, scatter), out_sha...]
    convert_element_type x1 -> x0, other arithmetic: 0.84 us -> none  [on_device(): jnp.pad(band_id, (HALO, TILE), constant_values=-1).astype(jnp.float32)]
where the time goes in v2:
time: 28.3 us; the launch traced here: 28.1 us
  Pallas kernels  24.6 us (87%)
  local copies, waits for them, and re-layouts  2.87 us (10%)
  between operations  0.64 us (2%)
    pallas_call x1, Pallas kernels, on_device(): pl.pallas_call(functools.partial(kernel, n_obs, n_chan, scatter), out_sha...  24.6 us
    unnamed x2, local copies, waits for them, and re-layouts  2.87 us

profile of v2, /device:TPU:0, one launch (start us, length us, event | category | flops | bytes accessed | tf_op | source)
XLA Modules:
  0.0 28.1 jit_solution(932412874091482988)
XLA Ops:
  0.6 24.6 %normal_equations.1 = (f32[100,256]{1,0:T(8,128)}, f32[10,256]{1,0:T(8,128)}) custom-call(bf16[2048,2048]{1,0:T(8,128)(2,1)} %dep.1, bf16[10,2048]{1,0:T(8,128)(2,1)} %pred_.1, bf16[63,2048]{1,0:T(8,128)(2,1)} %inv.1, s32[1,8192]{1,0:T(1,128)} %bitcast.1, s32[16]{0:T(128)} %counts.1), custom_call_target="tpu_custom_call" | custom-call | tf_op jit(solution)/shard_map/normal_equations/pallas_call | solution.py:367
  25.2 1.5 %copy.9 = f32[100,256]{1,0:T(8,128)} copy(f32[100,256]{1,0:T(8,128)} %get-tuple-element.4) | data formatting | bytes 204800
  26.8 1.3 %copy.10 = f32[10,256]{1,0:T(8,128)} copy(f32[10,256]{1,0:T(8,128)} %get-tuple-element.5) | data formatting | bytes 20480

commit v3 on v2

--- a/solution.py
+++ b/solution.py
@@ -12,7 +12,7 @@
 LANES = 128
 HALO = 32
 TILE = 128
-OBS_CHUNK = 512
+OBS_CHUNK = 1024
 MESH = pl.DeviceIdType.MESH
 
 
@@ -84,9 +84,16 @@
     def level_at(turn):
         return lax.rem(lev + stride * (turn + 1), pairs)
 
+    def for_partner(step):
+        odd = lax.rem(step, 2) == 1
+        return jnp.logical_or(step == 0, jnp.logical_and(odd, step < blocks - 1))
+
+    def turn_at(step):
+        return jnp.where(for_partner(step), lax.div(step + 1, 2), lax.div(jnp.maximum(step - 1, 0), 2))
+
     def block_at(step):
-        side = jnp.where(step < pairs, 1 - col, col)
-        return 2 * level_at(lax.rem(step, pairs)) + side
+        side = jnp.where(for_partner(step), 1 - col, col)
+        return 2 * level_at(turn_at(step)) + side
 
     barrier = pltpu.get_barrier_semaphore()
     for index in (left, right):
@@ -204,13 +211,13 @@
 
     flip[...] = jnp.zeros_like(flip)
 
-    def build(group, carry):
-        for lane_of in range(flip.shape[0]):
-            first = pl.multiple_of((group * flip.shape[0] + lane_of) * TILE, TILE)
+    def build(block):
+        for part in range(tiles):
+            first = pl.multiple_of(block * width + part * TILE, TILE)
             near = ids_in[:, pl.ds(first, 3 * TILE)].astype(jnp.float32)
-            flip[lane_of, 0:offsets, :] = inv_in[:, pl.ds(first, TILE)].astype(jnp.float32)
-            flip[lane_of, 64:65, :] = near[:, TILE : 2 * TILE]
-            turned = flip[lane_of].T
+            flip[part, 0:offsets, :] = inv_in[:, pl.ds(first, TILE)].astype(jnp.float32)
+            flip[part, 64:65, :] = near[:, TILE : 2 * TILE]
+            turned = flip[part].T
             own_id = turned[:, 64:65]
             place = lax.broadcasted_iota(jnp.int32, turned.shape, 1)
             turned = jnp.where(place < offsets, turned, 0.0)
@@ -222,10 +229,9 @@
                 stride_axis=0,
             )
             same = near[:, TILE - HALO : 3 * TILE - HALO] == own_id
-            bands[pl.ds(first, TILE), :] = jnp.where(same, skewed, 0.0).astype(jnp.bfloat16)
-        return carry
-
-    lax.fori_loop(0, own // TILE // flip.shape[0], build, 0)
+            bands[part * TILE : (part + 1) * TILE, :] = jnp.where(same, skewed, 0.0).astype(
+                jnp.bfloat16
+            )
 
     def send_x(turn):
         return pltpu.make_async_remote_copy(
@@ -258,18 +264,22 @@
             device_id_type=MESH,
         )
 
-    load(0).wait()
+    for place in range(3):
+        load(place).wait()
+    build(block_at(0))
 
     def one_block(step, carry):
         block = block_at(step)
 
-        @pl.when(step < pairs)
-        def _():
-            load(2 * step + 1).wait()
-
-        @pl.when(step < pairs - 1)
-        def _():
-            load(2 * step + 2).wait()
+        @pl.when(step == 1)
+        def _():
+            for place in range(3, 5):
+                load(place).wait()
+
+        @pl.when(step == 2)
+        def _():
+            for place in range(5, blocks):
+                load(place).wait()
 
         @pl.when(block == blocks - 1)
         def _():
@@ -282,12 +292,13 @@
         start = pl.multiple_of(block * width, width)
         extent = TILE + 2 * HALO
         sums = jnp.zeros((width, LANES), jnp.float32)
+        matrices = [bands[part * TILE : (part + 1) * TILE, 0:extent] for part in range(tiles)]
         for at in range(0, obs_dev, OBS_CHUNK):
             parts = []
             for part in range(tiles):
                 first = pl.multiple_of(start + part * TILE, TILE)
                 weighted = jnp.dot(
-                    bands[pl.ds(first, TILE), 0:extent],
+                    matrices[part],
                     window[pl.ds(first, extent), at : at + OBS_CHUNK],
                     preferred_element_type=jnp.float32,
                 )
@@ -300,21 +311,22 @@
                 table[2 * at : 2 * (at + OBS_CHUNK), :],
                 preferred_element_type=jnp.float32,
             )
+        build(block_at(jnp.minimum(step + 1, blocks - 1)))
         result = sums.T[:rows, :]
         if not scatter:
             part_out[:, pl.ds(start, width)] = result
             return carry
-        turn = lax.rem(step, pairs)
-
-        @pl.when(step < pairs)
-        def _():
-            stage[step] = result
+        turn = turn_at(step)
+
+        @pl.when(for_partner(step))
+        def _():
+            stage[turn] = result
             send_x(turn).start()
 
-        @pl.when(step >= pairs)
+        @pl.when(jnp.logical_not(for_partner(step)))
         def _():
             send_x(turn).wait_recv()
-            stage[step] = result + landed_x[turn]
+            stage[pairs + turn] = result + landed_x[turn]
 
             @pl.when(step < blocks - 1)
             def _():
@@ -354,8 +366,8 @@
     rows = -(-(upper + preds) // 8) * 8
     if scatter:
         out_shape = (
-            jax.ShapeDtypeStruct((preds * preds, share), jnp.float32),
-            jax.ShapeDtypeStruct((preds, share), jnp.float32),
+            pltpu.VMEM((preds * preds, share), jnp.float32),
+            pltpu.VMEM((preds, share), jnp.float32),
         )
     else:
         out_shape = (jax.ShapeDtypeStruct((rows, own), jnp.float32),)
@@ -377,8 +389,8 @@
             pltpu.SMEM(line_counts.shape, jnp.int32),
             pltpu.VMEM((LANES, obs_dev), jnp.float32),
             pltpu.VMEM((2 * obs_dev, LANES), jnp.bfloat16),
-            pltpu.VMEM((4, LANES, TILE), jnp.float32),
-            pltpu.VMEM((own, 2 * TILE), jnp.bfloat16),
+            pltpu.VMEM((width // TILE, LANES, TILE), jnp.float32),
+            pltpu.VMEM((width, 2 * TILE), jnp.bfloat16),
             pltpu.VMEM((blocks, rows, width), jnp.float32),
             pltpu.VMEM(landing, jnp.float32),
             pltpu.VMEM(landing, jnp.float32),
@@ -395,7 +407,7 @@
         compiler_params=pltpu.CompilerParams(
             collective_id=0,
             has_side_effects=True,
-            vmem_limit_bytes=67043328,
+            vmem_limit_bytes=67043328 - 120 * 1024,
         ),
         name="normal_equations",
     )(departures, predictors, inv_band, band_id[None, :], line_counts)

time: 28.3 us -> 24.1 us (0.85)
  Pallas kernels: 24.6 us -> 22.1 us
  local copies, waits for them, and re-layouts: 2.87 us -> 1.25 us
    pallas_call x1, Pallas kernels: 24.6 us -> 22.1 us  [on_device(): pl.pallas_call(functools.partial(kernel, n_obs, n_chan, scatter), out_sha...]
    unnamed x2, local copies, waits for them, and re-layouts: 2.87 us -> 1.25 us
where the time goes in v3:
time: 24.1 us; the launch traced here: 24 us
  Pallas kernels  22.1 us (92%)
  local copies, waits for them, and re-layouts  1.25 us (5%)
  between operations  0.64 us (3%)
    pallas_call x1, Pallas kernels, on_device(): pl.pallas_call(functools.partial(kernel, n_obs, n_chan, scatter), out_sha...  22.1 us
    unnamed x2, local copies, waits for them, and re-layouts  1.25 us

profile of v3, /device:TPU:0, one launch (start us, length us, event | category | flops | bytes accessed | tf_op | source)
XLA Modules:
  0.0 24.0 jit_solution(6866249864894882238)
XLA Ops:
  0.6 22.1 %normal_equations.1 = (f32[100,256]{1,0:T(8,128)S(1)}, f32[10,256]{1,0:T(8,128)S(1)}) custom-call(bf16[2048,2048]{1,0:T(8,128)(2,1)} %dep.1, bf16[10,2048]{1,0:T(8,128)(2,1)} %pred_.1, bf16[63,2048]{1,0:T(8,128)(2,1)} %inv.1, s32[1,8192]{1,0:T(1,128)} %bitcast.1, s32[16]{0:T(128)} %counts.1), custom_call_target="tpu_custom_call" | custom-call | tf_op jit(solution)/shard_map/normal_equations/pallas_call | solution.py:379
  22.7 0.6 %copy.9 = f32[100,256]{1,0:T(8,128)} copy(f32[100,256]{1,0:T(8,128)S(1)} %get-tuple-element.2) | data formatting | bytes 204800
  23.4 0.6 %copy.10 = f32[10,256]{1,0:T(8,128)} copy(f32[10,256]{1,0:T(8,128)S(1)} %get-tuple-element.3) | data formatting | bytes 20480

commit v4 on v3

--- a/solution.py
+++ b/solution.py
@@ -12,7 +12,7 @@
 LANES = 128
 HALO = 32
 TILE = 128
-OBS_CHUNK = 1024
+OBS_CHUNK = 2048
 MESH = pl.DeviceIdType.MESH
 
 
@@ -174,7 +174,7 @@
         )
         return carry
 
-    lax.fori_loop(0, lines, turn_line, 0, unroll=2)
+    lax.fori_loop(0, lines, turn_line, 0, unroll=4)
 
     pl.semaphore_wait(barrier, greeted)
     to_left = pltpu.make_async_remote_copy(

time: 24.1 us -> 23.6 us (0.979)
  Pallas kernels: 22.1 us -> 21.6 us
    pallas_call x1, Pallas kernels: 22.1 us -> 21.6 us  [on_device(): pl.pallas_call(functools.partial(kernel, n_obs, n_chan, scatter), out_sha...]
where the time goes in v4:
time: 23.6 us; the launch traced here: 23.5 us
  Pallas kernels  21.6 us (92%)
  local copies, waits for them, and re-layouts  1.25 us (5%)
  between operations  0.64 us (3%)
    pallas_call x1, Pallas kernels, on_device(): pl.pallas_call(functools.partial(kernel, n_obs, n_chan, scatter), out_sha...  21.6 us
    unnamed x2, local copies, waits for them, and re-layouts  1.25 us

profile of v4, /device:TPU:0, one launch (start us, length us, event | category | flops | bytes accessed | tf_op | source)
XLA Modules:
  0.0 23.5 jit_solution(2700838260960938131)
XLA Ops:
  0.6 21.6 %normal_equations.1 = (f32[100,256]{1,0:T(8,128)S(1)}, f32[10,256]{1,0:T(8,128)S(1)}) custom-call(bf16[2048,2048]{1,0:T(8,128)(2,1)} %dep.1, bf16[10,2048]{1,0:T(8,128)(2,1)} %pred_.1, bf16[63,2048]{1,0:T(8,128)(2,1)} %inv.1, s32[1,8192]{1,0:T(1,128)} %bitcast.1, s32[16]{0:T(128)} %counts.1), custom_call_target="tpu_custom_call" | custom-call | tf_op jit(solution)/shard_map/normal_equations/pallas_call | solution.py:379
  22.2 0.6 %copy.9 = f32[100,256]{1,0:T(8,128)} copy(f32[100,256]{1,0:T(8,128)S(1)} %get-tuple-element.2) | data formatting | bytes 204800
  22.9 0.6 %copy.10 = f32[10,256]{1,0:T(8,128)} copy(f32[10,256]{1,0:T(8,128)S(1)} %get-tuple-element.3) | data formatting | bytes 20480
